TPU v7x, 32 devices: a whole 2x2x4 slice. The times are simulated.
32 devices in a mesh: rows: 8 (over y, x, core), sub: 4 (over z).
Axes of the slice: x: 2, y: 2, z: 4, core: 2. Of those that a mesh axis runs over, the one named last changes fastest.
Arguments:
- u_fem: float32 [120, 524288], P(None, ('rows', 'sub')), may hold values from -600 to 600
- resid_fem: float32 [1, 524288], P(None, ('rows', 'sub')), may hold values from -60 to 60
- slot_map: int32 [32, 32], P(('rows', 'sub')), may hold values from 0 to 31, as said below
- restart: float32 [120, 40], replicated, may hold values from -0.5 to 0.5
- coeff: float32 [3, 120, 120], P(None, None, 'sub'), may hold values from -6 to 6
Outputs:
- new_basis: float32 [40, 524288], P(None, ('rows', 'sub'))
- next_vector: float32 [1, 524288], P(None, ('rows', 'sub'))
- new_coeff: float32 [3, 40, 120], replicated
Inputs may be any that keep to these rules, and one draw needn't show every extreme that they name: Each row of slot_map is a permutation of 0 to 31.
All inputs are finite; a program needn't handle non-finite values.
Results may differ from a plain program's by a relative error of at most 0.00015.
Values sent between devices are 32-bit elements; how exact they have to be, the bound alone decides.
A program may use at most 64 MiB of HBM per device.

v0:
```python
import jax
import jax.numpy as jnp
from jax import lax
from jax.sharding import PartitionSpec as P


def settle(values, source, dev_count):
    width = values.shape[0]
    block_len = values.shape[1] // dev_count
    blocks = values.reshape(width, dev_count, block_len)
    return jnp.take(blocks, source, axis=1).reshape(width, dev_count * block_len)


def local(u_fem, resid_fem, slot_map, restart, coeff):
    highest = lax.Precision.HIGHEST
    dev_count = lax.axis_size(("rows", "sub"))
    nrows_all = u_fem.shape[1] * dev_count
    source = jnp.argsort(slot_map[0])
    basis_rows, resid_row = (u_fem, resid_fem)
    gram_local = jnp.einsum("kn,jn->kj", basis_rows, basis_rows, precision=highest)
    inner_local = jnp.einsum("kn,n->k", basis_rows, resid_row[0], precision=highest)
    gram_sum = lax.psum(gram_local, ("rows", "sub"))
    chol_lower = jnp.linalg.cholesky(gram_sum / nrows_all)
    factor = lax.linalg.triangular_solve(
        chol_lower, restart, left_side=True, lower=True, transpose_a=True
    )
    new_rows = jnp.einsum("kp,kn->pn", factor, basis_rows, precision=highest)
    inner_prod = lax.psum(inner_local, ("rows", "sub"))
    half_solve = lax.linalg.triangular_solve(
        chol_lower, inner_prod[:, None], left_side=True, lower=True
    )
    proj_coef = (
        lax.linalg.triangular_solve(
            chol_lower, half_solve, left_side=True, lower=True, transpose_a=True
        )[:, 0]
        / nrows_all
    )
    remainder = resid_row - jnp.einsum("k,kn->n", proj_coef, basis_rows, precision=highest)[None, :]
    norm_sum = lax.psum(jnp.sum(remainder * remainder), ("rows", "sub"))
    next_row = remainder * lax.rsqrt(norm_sum / nrows_all + 1e-06)
    new_rows, next_row = (
        lax.all_to_all(new_rows, ("rows", "sub"), split_axis=1, concat_axis=1, tiled=True),
        lax.all_to_all(next_row, ("rows", "sub"), split_axis=1, concat_axis=1, tiled=True),
    )
    new_rows = settle(new_rows, source, dev_count)
    next_row = settle(next_row, source, dev_count)
    raised = jnp.dot(chol_lower, restart, precision=highest)
    coeff_all = lax.all_gather(coeff, "sub", axis=2, tiled=True)
    rotated = jnp.einsum("kp,ikm->ipm", raised, coeff_all, precision=highest)
    new_coeff = rotated * lax.rsqrt(jnp.mean(rotated * rotated) + 1e-06)
    return (new_rows, next_row, new_coeff)


def solution(mesh):
    in_specs = (
        P(None, ("rows", "sub")),
        P(None, ("rows", "sub")),
        P(("rows", "sub"), None),
        P(),
        P(None, None, "sub"),
    )
    out_specs = (P(None, ("rows", "sub")), P(None, ("rows", "sub")), P())
    return jax.shard_map(local, mesh=mesh, in_specs=in_specs, out_specs=out_specs, check_vma=False)
```

profile of v0, /device:TPU:0, one launch (start us, length us, event | category | flops | bytes accessed | tf_op | source)
XLA Modules:
  0.0 229.9 jit_solution(9403381852364649270)
XLA Ops:
  0.7 10.1 %fusion.16 = f32[120,120]{0,1:T(8,128)S(1)} fusion(f32[120,16384]{1,0:T(8,128)} %param.5), kind=kOutput, calls=%fused_computation.44 | convolution fusion | flops 2831155200 | bytes 7921920 | tf_op jit(solution)/shard_map/kn,jn->kj/dot_general | solution.py:20
  10.8 6.2 %convolution_bitcast_fusion.3 = f32[120]{0:T(128)S(1)} fusion(f32[120,16384]{1,0:T(8,128)S(1)} %copy-done.1, f32[1,16384]{1,0:T(1,128)S(1)} %copy-done.2), kind=kOutput, calls=%fused_computation.10 | convolution fusion | flops 23592960 | bytes 7930336 | tf_op jit(solution)/shard_map/kn,n->k/dot_general | solution.py:21
  16.9 42.8 %all-reduce = (f32[120,120]{0,1:T(8,128)S(1)}, f32[120]{0:T(128)S(1)}) all-reduce(f32[120,120]{0,1:T(8,128)S(1)} %fusion.16, f32[120]{0:T(128)S(1)} %convolution_bitcast_fusion.3), channel_id=1, replica_groups=mesh['rows'=8,'sub'=4] {'rows','sub'}, use_global_device_ids=true, to_apply=%region_1.2 | all-reduce | flops 14520 | bytes 116160 | tf_op jit(solution)/shard_map/psum | solution.py:22
  59.8 0.1 copy.18
  59.9 11.0 %cholesky.16 = f32[120,120]{1,0:T(8,128)S(1)} custom-call(f32[120,120]{1,0:T(8,128)S(1)} %fusion.9), custom_call_target="Cholesky" | custom-call | tf_op jit(solution)/shard_map/jit(cholesky)/cholesky | solution.py:23
  70.9 0.6 compare_reduce_fusion
  71.5 0.7 select_bitcast_fusion
  72.2 9.2 %custom-call.10 = f32[1,120,120]{1,2,0:T(8,128)S(1)} custom-call(f32[1,120,120]{2,1,0:T(8,128)S(1)} %select_bitcast_fusion), custom_call_target="InvertDiagBlocksLowerTriangular" | custom-call | tf_op jit(solution)/shard_map/triangular_solve | solution.py:24
  81.4 0.2 convolution_bitcast_fusion.2
  81.6 0.2 fusion.1
  81.8 6.7 %multiply_reduce_fusion = (f32[]{:T(128)}, f32[1,16384]{1,0:T(1,128)S(1)}) fusion(f32[1,16384]{1,0:T(1,128)S(1)} %copy-done.2, f32[120,1]{0,1:T(1,128)S(1)} %fusion.1, f32[120,16384]{1,0:T(8,128)} %param.5), kind=kOutput, calls=%fused_computation.15 | convolution fusion | flops 23642112 | bytes 7995876 | tf_op jit(solution)/shard_map/k,kn->n/dot_general | solution.py:38
  88.5 40.3 %psum.23 = f32[]{:T(128)} all-reduce(f32[]{:T(128)} %get-tuple-element.7), channel_id=1, replica_groups=mesh['rows'=8,'sub'=4] {'rows','sub'}, use_global_device_ids=true, to_apply=%region_6.7 | all-reduce | flops 1 | bytes 8 | tf_op jit(solution)/shard_map/psum | solution.py:39
  129.5 0.7 broadcast_multiply_fusion
  130.1 5.4 %all-to-all-start.1 = ((f32[1,32,512]{2,0,1:T(1,128)}), f32[1,32,512]{2,0,1:T(1,128)S(1)}, u32[]{:S(2)}, u32[]{:S(2)}) async-start(f32[1,32,512]{2,0,1:T(1,128)} %bitcast.14), calls=%async_computation.1 | async-start | bytes 131072 | tf_op jit(solution)/shard_map/all_to_all | solution.py:43
  135.6 0.2 fusion.7
  135.8 6.5 %fusion.17 = f32[40,16384]{1,0:T(8,128)S(1)} fusion(f32[120,40]{0,1:T(8,128)S(1)} %fusion.7, f32[120,16384]{1,0:T(8,128)} %param.5), kind=kOutput, calls=%fused_computation.45 | convolution fusion | flops 943718400 | bytes 10504960 | tf_op jit(solution)/shard_map/kp,kn->pn/dot_general | solution.py:27
  142.3 1.7 copy.36
  144.1 1.7 sort.17
  145.8 5.8 %all-to-all-start = ((f32[40,32,512]{2,0,1:T(8,128)}), f32[40,32,512]{2,0,1:T(8,128)S(1)}, u32[]{:S(2)}, u32[]{:S(2)}) async-start(f32[40,32,512]{2,0,1:T(8,128)} %bitcast.69), calls=%async_computation | async-start | bytes 5242880 | tf_op jit(solution)/shard_map/all_to_all | solution.py:42
  151.6 0.1 broadcast_bitcast_fusion
  151.7 0.1 copy.28
  151.8 67.3 %all_gather.3 = f32[3,120,120]{1,0,2:T(4,128)S(1)} all-gather(f32[3,120,30]{1,0,2:T(4,128)S(1)} %copy.21), channel_id=1, replica_groups=mesh['rows'=8,'sub'=4] {'sub'}, dimensions={2}, use_global_device_ids=true | all-gather | bytes 216000 | tf_op jit(solution)/shard_map/all_gather | solution.py:48
  219.1 0.9 convolution_bitcast_fusion
  220.0 1.0 multiply_reduce_fusion.1
  221.8 0.1 broadcast_bitcast_fusion.1
  221.9 0.6 multiply_bitcast_fusion
  222.5 0.6 gather_fusion.1
  223.1 0.1 copy.29
  223.2 0.7 broadcast_select_fusion.1
  223.9 2.2 gather_fusion
  226.2 2.1 copy.26
  228.2 1.7 broadcast_select_fusion
  (22 shorter events, 0.2 us)
Async XLA Ops:
  0.6 134.9 %copy-start = (f32[120,40]{0,1:T(8,128)S(1)}, f32[120,40]{0,1:T(8,128)}, u32[]{:S(2)}) copy-start(f32[120,40]{0,1:T(8,128)} %param.8) | copy-start | bytes 57604
  0.6 10.1 %copy-start.1 = (f32[120,16384]{1,0:T(8,128)S(1)}, f32[120,16384]{1,0:T(8,128)}, u32[]{:S(2)}) copy-start(f32[120,16384]{1,0:T(8,128)} %param.5) | copy-start | bytes 23592964
  0.7 10.1 %copy-start.2 = (f32[1,16384]{1,0:T(1,128)S(1)}, f32[1,16384]{1,0:T(1,128)}, u32[]{:S(2)}) copy-start(f32[1,16384]{1,0:T(1,128)} %param.6) | copy-start | bytes 196612
  130.1 15.6 %all-to-all-start.1 = ((f32[1,32,512]{2,0,1:T(1,128)}), f32[1,32,512]{2,0,1:T(1,128)S(1)}, u32[]{:S(2)}, u32[]{:S(2)}) async-start(f32[1,32,512]{2,0,1:T(1,128)} %bitcast.14), calls=%async_computation.1 | async-start | bytes 131072 | tf_op jit(solution)/shard_map/all_to_all | solution.py:43
  135.8 8.3 %copy-start.4 = (s32[1,32]{1,0:T(1,128)S(1)}, s32[1,32]{1,0:T(1,128)}, u32[]{:S(2)}) copy-start(s32[1,32]{1,0:T(1,128)} %param.7) | copy-start | bytes 388
  142.3 9.4 %copy-start.3 = (f32[3,120,30]{1,2,0:T(8,128)S(1)}, f32[3,120,30]{1,2,0:T(8,128)}, u32[]{:S(2)}) copy-start(f32[3,120,30]{1,2,0:T(8,128)} %param.9) | copy-start | bytes 129604
  145.8 78.2 %all-to-all-start = ((f32[40,32,512]{2,0,1:T(8,128)}), f32[40,32,512]{2,0,1:T(8,128)S(1)}, u32[]{:S(2)}, u32[]{:S(2)}) async-start(f32[40,32,512]{2,0,1:T(8,128)} %bitcast.69), calls=%async_computation | async-start | bytes 5242880 | tf_op jit(solution)/shard_map/all_to_all | solution.py:42
where the time goes:
time: 231 us; the launch traced here: 230 us
  blocking collectives  150 us (65%)
  matrix products  32 us (14%)
  other arithmetic  27 us (12%)
  starting transfers between devices  11.2 us (5%)
  local copies, waits for them, and re-layouts  7.06 us (3%)
    all_gather x1, blocking collectives, local(): coeff_all = lax.all_gather(coeff, 'sub', axis=2, tiled=True)  67.3 us
    psum x1, blocking collectives, local(): gram_sum = lax.psum(gram_local, ('rows', 'sub'))  42.8 us
    psum x1, blocking collectives, local(): norm_sum = lax.psum(jnp.sum(remainder * remainder), ('rows', 'sub'))  40.3 us
    another operation x3, other arithmetic, local(): chol_lower = jnp.linalg.cholesky(gram_sum / nrows_all)  11.6 us
    dot_general x1, matrix products, local(): jnp.einsum('kn,jn->kj', basis_rows, basis_rows, precision=highest)  10.1 us
    another operation x2, other arithmetic, local(): lax.linalg.triangular_solve(chol_lower, restart, left_side=True, lower=Tr...  9.85 us
    dot_general x1, matrix products, local(): jnp.einsum('k,kn->n', proj_coef, basis_rows, precision=highest)[None, :]  6.74 us
    dot_general x1, matrix products, local(): new_rows = jnp.einsum('kp,kn->pn', factor, basis_rows, precision=highest)  6.51 us
  transfers between devices with their start and end apart: 2, of which 0 were waited for; matrix products, arithmetic and copies ran while one was open for 6% of the time, Pallas kernels for 0%

commit v1 on v0

--- a/solution.py
+++ b/solution.py
@@ -2,6 +2,15 @@
 import jax.numpy as jnp
 from jax import lax
 from jax.sharding import PartitionSpec as P
+
+
+def build_patch_on(own_rows, axis_no):
+    own_rows = jnp.moveaxis(own_rows, 0, axis_no)
+    local_out = own_rows.shape
+    y_new = own_rows.reshape(
+        *local_out[:axis_no], local_out[axis_no] * local_out[axis_no + 1], *local_out[axis_no + 2 :]
+    )
+    return y_new
 
 
 def settle(values, source, dev_count):
@@ -45,8 +54,28 @@
     new_rows = settle(new_rows, source, dev_count)
     next_row = settle(next_row, source, dev_count)
     raised = jnp.dot(chol_lower, restart, precision=highest)
-    coeff_all = lax.all_gather(coeff, "sub", axis=2, tiled=True)
-    rotated = jnp.einsum("kp,ikm->ipm", raised, coeff_all, precision=highest)
+    opened = lax.psum(1, axis_name="sub")
+    mat_out, all_rows, main = (opened, lax.axis_index("sub"), coeff.shape[2])
+    gallery = tuple(((rr, (rr + 1) % mat_out) for rr in range(mat_out)))
+    in_order = tuple(((rr, (rr - 1) % mat_out) for rr in range(mat_out)))
+    k_now = mat_out // 2
+    passed = {}
+    b_now = item_now = coeff
+    for dd in [*range(k_now + 1)]:
+        ready = lax.ppermute(b_now, axis_name="sub", perm=gallery) if dd < k_now else None
+        high = (
+            lax.ppermute(item_now, axis_name="sub", perm=in_order)
+            if dd < mat_out - k_now - 1
+            else None
+        )
+        passed[-dd] = jnp.einsum("kp,ikm->ipm", raised, b_now, precision=highest)
+        if 0 < dd < mat_out - k_now:
+            passed[dd] = jnp.einsum("kp,ikm->ipm", raised, item_now, precision=highest)
+        b_now, item_now = (ready, high)
+    t1 = tuple((passed[hop_no] for hop_no in sorted(passed)))
+    passed = jnp.stack(t1, axis=0)
+    passed = passed[(jnp.arange(mat_out) - all_rows + k_now) % mat_out]
+    rotated = build_patch_on(passed, 2)
     new_coeff = rotated * lax.rsqrt(jnp.mean(rotated * rotated) + 1e-06)
     return (new_rows, next_row, new_coeff)
 

time: 231 us -> 223 us (0.965)
  blocking collectives: 150 us -> 80.3 us
  waiting for transfers between devices: 0.01 us -> 52.6 us
  starting transfers between devices: 11.2 us -> 18.1 us
    all_gather x1 -> x0, blocking collectives: 67.3 us -> none  [local(): coeff_all = lax.all_gather(coeff, 'sub', axis=2, tiled=True)]
    ppermute x0 -> x3, waiting for transfers between devices: none -> 46.4 us  [the longest x2 46.4 us: local(): lax.ppermute(b_now, axis_name='sub', perm=gallery)]
    ppermute x0 -> x3, starting transfers between devices: none -> 7.02 us  [the longest x2 4.93 us: local(): lax.ppermute(b_now, axis_name='sub', perm=gallery)]
    all_to_all x1, waiting for transfers between devices: 0.01 us -> 6.25 us  [local(): lax.all_to_all(new_rows, ('rows', 'sub'), split_axis=1, concat_axis=1, ti...]
    psum x1, blocking collectives: 42.8 us -> 39.8 us  [local(): gram_sum = lax.psum(gram_local, ('rows', 'sub'))]
  transfers between devices with their start and end apart: 2 -> 5, of which waited for: 0 -> 2; matrix products, arithmetic and copies ran while one was open for 6% -> 28% of each run, Pallas kernels for 0% -> 0%
where the time goes in v1:
time: 223 us; the launch traced here: 220 us
  blocking collectives  80.3 us (36%)
  waiting for transfers between devices  52.6 us (24%)
  matrix products  31.6 us (14%)
  other arithmetic  27 us (12%)
  starting transfers between devices  18.1 us (8%)
  local copies, waits for them, and re-layouts  8.45 us (4%)
  between operations  2.31 us (1%)
    ppermute x2, waiting for transfers between devices, local(): lax.ppermute(b_now, axis_name='sub', perm=gallery)  46.4 us
    psum x1, blocking collectives, local(): norm_sum = lax.psum(jnp.sum(remainder * remainder), ('rows', 'sub'))  40.4 us
    psum x1, blocking collectives, local(): gram_sum = lax.psum(gram_local, ('rows', 'sub'))  39.8 us
    another operation x3, other arithmetic, local(): chol_lower = jnp.linalg.cholesky(gram_sum / nrows_all)  11.6 us
    dot_general x1, matrix products, local(): jnp.einsum('kn,jn->kj', basis_rows, basis_rows, precision=highest)  9.92 us
    another operation x2, other arithmetic, local(): lax.linalg.triangular_solve(chol_lower, restart, left_side=True, lower=Tr...  9.85 us
    dot_general x1, matrix products, local(): jnp.einsum('k,kn->n', proj_coef, basis_rows, precision=highest)[None, :]  6.74 us
    dot_general x1, matrix products, local(): new_rows = jnp.einsum('kp,kn->pn', factor, basis_rows, precision=highest)  6.51 us
  transfers between devices with their start and end apart: 5, of which 2 were waited for; matrix products, arithmetic and copies ran while one was open for 28% of the time, Pallas kernels for 0%

profile of v1, /device:TPU:0, one launch (start us, length us, event | category | flops | bytes accessed | tf_op | source)
XLA Modules:
  0.0 220.3 jit_solution(1766234675541413213)
XLA Ops:
  0.7 3.1 %collective-permute-start = (f32[3,120,30]{1,2,0:T(8,128)}, f32[3,120,30]{1,2,0:T(8,128)S(1)}, u32[]{:S(2)}, u32[]{:S(2)}) collective-permute-start(f32[3,120,30]{1,2,0:T(8,128)} %param.9), channel_id=1, source_target_pairs={{0,1},{1,2},{2,3},{3,0},{4,5},{5,6},{6,7},{7,4},{8,9},{9,10},{10,1... | collective-permute-start | bytes 129608 | tf_op jit(solution)/shard_map/ppermute | solution.py:65
  3.8 2.1 collective-permute-start.2
  5.9 9.9 %fusion.16 = f32[120,120]{0,1:T(8,128)S(1)} fusion(f32[120,16384]{1,0:T(8,128)} %param.5), kind=kOutput, calls=%fused_computation.55 | convolution fusion | flops 2831155200 | bytes 7921920 | tf_op jit(solution)/shard_map/kn,jn->kj/dot_general | solution.py:29
  15.8 6.2 %convolution_bitcast_fusion.7 = f32[120]{0:T(128)S(1)} fusion(f32[120,16384]{1,0:T(8,128)S(1)} %copy-done.1, f32[1,16384]{1,0:T(1,128)S(1)} %copy-done.2), kind=kOutput, calls=%fused_computation.15 | convolution fusion | flops 23592960 | bytes 7930336 | tf_op jit(solution)/shard_map/kn,n->k/dot_general | solution.py:30
  22.0 39.8 %all-reduce = (f32[120,120]{0,1:T(8,128)S(1)}, f32[120]{0:T(128)S(1)}) all-reduce(f32[120,120]{0,1:T(8,128)S(1)} %fusion.16, f32[120]{0:T(128)S(1)} %convolution_bitcast_fusion.7), channel_id=1, replica_groups=mesh['rows'=8,'sub'=4] {'rows','sub'}, use_global_device_ids=true, to_apply=%region_1.2 | all-reduce | flops 14520 | bytes 116160 | tf_op jit(solution)/shard_map/psum | solution.py:31
  62.0 11.0 %cholesky.16 = f32[120,120]{1,0:T(8,128)S(1)} custom-call(f32[120,120]{1,0:T(8,128)S(1)} %fusion.7), custom_call_target="Cholesky" | custom-call | tf_op jit(solution)/shard_map/jit(cholesky)/cholesky | solution.py:32
  73.0 0.6 compare_reduce_fusion
  73.6 0.7 select_bitcast_fusion
  74.3 9.2 %custom-call.10 = f32[1,120,120]{1,2,0:T(8,128)S(1)} custom-call(f32[1,120,120]{2,1,0:T(8,128)S(1)} %select_bitcast_fusion), custom_call_target="InvertDiagBlocksLowerTriangular" | custom-call | tf_op jit(solution)/shard_map/triangular_solve | solution.py:33
  83.7 0.2 fusion.1
  83.9 6.7 %multiply_reduce_fusion.1 = (f32[]{:T(128)}, f32[1,16384]{1,0:T(1,128)S(1)}) fusion(f32[1,16384]{1,0:T(1,128)S(1)} %copy-done.2, f32[120,1]{0,1:T(1,128)S(1)} %fusion.1, f32[120,16384]{1,0:T(8,128)} %param.5), kind=kOutput, calls=%fused_computation.21 | convolution fusion | flops 23642112 | bytes 7995876 | tf_op jit(solution)/shard_map/k,kn->n/dot_general | solution.py:47
  90.6 40.4 %psum.23 = f32[]{:T(128)} all-reduce(f32[]{:T(128)} %get-tuple-element.7), channel_id=1, replica_groups=mesh['rows'=8,'sub'=4] {'rows','sub'}, use_global_device_ids=true, to_apply=%region_6.7 | all-reduce | flops 1 | bytes 8 | tf_op jit(solution)/shard_map/psum | solution.py:48
  131.7 0.7 broadcast_multiply_fusion
  132.4 5.4 %all-to-all-start.1 = ((f32[1,32,512]{2,0,1:T(1,128)}), f32[1,32,512]{2,0,1:T(1,128)S(1)}, u32[]{:S(2)}, u32[]{:S(2)}) async-start(f32[1,32,512]{2,0,1:T(1,128)} %bitcast.14), calls=%async_computation.1 | async-start | bytes 131072 | tf_op jit(solution)/shard_map/all_to_all | solution.py:52
  137.8 1.6 sort.17
  139.5 0.2 fusion.5
  139.7 6.5 %fusion.17 = f32[40,16384]{1,0:T(8,128)S(1)} fusion(f32[120,40]{0,1:T(8,128)S(1)} %fusion.5, f32[120,16384]{1,0:T(8,128)} %param.5), kind=kOutput, calls=%fused_computation.56 | convolution fusion | flops 943718400 | bytes 10504960 | tf_op jit(solution)/shard_map/kp,kn->pn/dot_general | solution.py:36
  146.3 0.9 convolution_bitcast_fusion.4
  147.2 1.7 copy.33
  149.1 5.6 %all-to-all-start = ((f32[40,32,512]{2,0,1:T(8,128)}), f32[40,32,512]{2,0,1:T(8,128)S(1)}, u32[]{:S(2)}, u32[]{:S(2)}) async-start(f32[40,32,512]{2,0,1:T(8,128)} %bitcast.94), calls=%async_computation | async-start | bytes 5242880 | tf_op jit(solution)/shard_map/all_to_all | solution.py:51
  155.0 1.8 collective-permute-start.1
  157.0 0.2 convolution_bitcast_fusion
  157.2 46.4 %collective-permute-done.1 = f32[3,120,30]{1,2,0:T(8,128)S(1)} collective-permute-done((f32[3,120,30]{1,2,0:T(8,128)S(1)}, f32[3,120,30]{1,2,0:T(8,128)S(1)}, u32[]{:S(2)}, u32[]{:S(2)}) %collective-permute-start.1) | collective-permute-done | bytes 43232 | tf_op jit(solution)/shard_map/ppermute | solution.py:65
  203.8 0.6 gather_fusion.2
  204.4 0.7 multiply_reduce_fusion
  205.9 0.8 mul.33
  206.7 0.6 gather_fusion.1
  207.4 0.7 broadcast_select_fusion.1
  208.1 6.2 %all-to-all-done = f32[40,32,512]{2,0,1:T(8,128)S(1)} async-done(((f32[40,32,512]{2,0,1:T(8,128)}), f32[40,32,512]{2,0,1:T(8,128)S(1)}, u32[]{:S(2)}, u32[]{:S(2)}) %all-to-all-start) | async-done | bytes 2621472 | tf_op jit(solution)/shard_map/all_to_all | solution.py:51
  214.4 2.2 %gather_fusion = f32[32,40,512]{2,1,0:T(8,128)} fusion(f32[40,32,512]{2,0,1:T(8,128)S(1)} %all-to-all-done, s32[1024]{0:T(1024)S(1)} %pad_clamp_fusion.1), kind=kCustom, calls=%fused_computation | custom fusion | bytes 5243008 | tf_op jit(solution)/shard_map/jit(_take)/gather | solution.py:20
  216.6 2.0 copy.27
  218.6 1.7 broadcast_select_fusion
  (36 shorter events, 1.4 us)
Async XLA Ops:
  0.6 138.8 %copy-start = (f32[120,40]{0,1:T(8,128)S(1)}, f32[120,40]{0,1:T(8,128)}, u32[]{:S(2)}) copy-start(f32[120,40]{0,1:T(8,128)} %param.8) | copy-start | bytes 57604
  0.6 15.2 %copy-start.1 = (f32[120,16384]{1,0:T(8,128)S(1)}, f32[120,16384]{1,0:T(8,128)}, u32[]{:S(2)}) copy-start(f32[120,16384]{1,0:T(8,128)} %param.5) | copy-start | bytes 23592964
  0.7 15.1 %copy-start.2 = (f32[1,16384]{1,0:T(1,128)S(1)}, f32[1,16384]{1,0:T(1,128)}, u32[]{:S(2)}) copy-start(f32[1,16384]{1,0:T(1,128)} %param.6) | copy-start | bytes 196612
  0.7 154.4 %collective-permute-start = (f32[3,120,30]{1,2,0:T(8,128)}, f32[3,120,30]{1,2,0:T(8,128)S(1)}, u32[]{:S(2)}, u32[]{:S(2)}) collective-permute-start(f32[3,120,30]{1,2,0:T(8,128)} %param.9), channel_id=1, source_target_pairs={{0,1},{1,2},{2,3},{3,0},{4,5},{5,6},{6,7},{7,4},{8,9},{9,10},{10,1... | collective-permute-start | bytes 129608 | tf_op jit(solution)/shard_map/ppermute | solution.py:65
  3.8 153.3 %collective-permute-start.2 = (f32[3,120,30]{1,2,0:T(8,128)}, f32[3,120,30]{1,2,0:T(8,128)S(1)}, u32[]{:S(2)}, u32[]{:S(2)}) collective-permute-start(f32[3,120,30]{1,2,0:T(8,128)} %param.9), channel_id=1, source_target_pairs={{0,3},{1,0},{2,1},{3,2},{4,7},{5,4},{6,5},{7,6},{8,11},{9,8},{10,9... | collective-permute-start | bytes 129608 | tf_op jit(solution)/shard_map/ppermute | solution.py:67
  15.8 122.0 %copy-start.4 = (s32[1,32]{1,0:T(1,128)S(1)}, s32[1,32]{1,0:T(1,128)}, u32[]{:S(2)}) copy-start(s32[1,32]{1,0:T(1,128)} %param.7) | copy-start | bytes 388
  132.4 16.7 %all-to-all-start.1 = ((f32[1,32,512]{2,0,1:T(1,128)}), f32[1,32,512]{2,0,1:T(1,128)S(1)}, u32[]{:S(2)}, u32[]{:S(2)}) async-start(f32[1,32,512]{2,0,1:T(1,128)} %bitcast.14), calls=%async_computation.1 | async-start | bytes 131072 | tf_op jit(solution)/shard_map/all_to_all | solution.py:52
  139.7 9.2 %copy-start.3 = (f32[3,120,30]{1,2,0:T(8,128)S(1)}, f32[3,120,30]{1,2,0:T(8,128)}, u32[]{:S(2)}) copy-start(f32[3,120,30]{1,2,0:T(8,128)} %param.9) | copy-start | bytes 129604
  149.1 65.3 %all-to-all-start = ((f32[40,32,512]{2,0,1:T(8,128)}), f32[40,32,512]{2,0,1:T(8,128)S(1)}, u32[]{:S(2)}, u32[]{:S(2)}) async-start(f32[40,32,512]{2,0,1:T(8,128)} %bitcast.94), calls=%async_computation | async-start | bytes 5242880 | tf_op jit(solution)/shard_map/all_to_all | solution.py:51
  155.0 48.6 %collective-permute-start.1 = (f32[3,120,30]{1,2,0:T(8,128)S(1)}, f32[3,120,30]{1,2,0:T(8,128)S(1)}, u32[]{:S(2)}, u32[]{:S(2)}) collective-permute-start(f32[3,120,30]{1,2,0:T(8,128)S(1)} %collective-permute-done), channel_id=1, source_target_pairs={{0,1},{1,2},{2,3},{3,0},{4,5},{5,6},{6,7},{7,4},{8,9},{9,10},{10,1... | collective-permute-start | bytes 129608 | tf_op jit(solution)/shard_map/ppermute | solution.py:65
